TPU v7x, 128 devices: a whole 4x4x4 slice. The times are simulated.
128 devices in a mesh: band: 8 (over x, core), grid: 16 (over z, y).
Axes of the slice: x: 4, y: 4, z: 4, core: 2. Of those that a mesh axis runs over, the one named last changes fastest.
Arguments:
- orbitals: bfloat16 [32768, 2048], P('grid', 'band'), may hold values from -6 to 6
- projectors: bfloat16 [128, 8, 128], replicated, may hold values from -0.5 to 0.5
- sphere_start: int32 [128], replicated, may hold values from 0 to 1920, as said below
- proj_count: int32 [128], replicated, may hold values from 1 to 8
- owner_slab: int32 [128], replicated, may hold values from 0 to 15, as said below
- correlation_coef: float32 [128, 8, 8], replicated, as said below
Outputs:
- rotated: bfloat16 [32768, 2048], P(('grid', 'band'))
Inputs may be any that keep to these rules, and one draw needn't show every extreme that they name: `sphere_start`: a multiple of 128. `owner_slab`: every slab owns exactly 8 atoms. `correlation_coef`: each atom's matrix is symmetric positive definite.
All inputs are finite; a program needn't handle non-finite values.
Results may differ from a plain program's by a relative error of at most 0.0049.
Values may be sent and summed in bfloat16 or wider, within the bound.
A program may use at most 128 MiB of HBM per device.

v0:
```python
import jax
import jax.numpy as jnp
from jax import lax
from jax.sharding import PartitionSpec as P

SPH = 128
NPMAX = 8
A_SLAB = 8


def inverse_factor(matrix):
    order = matrix.shape[0]
    if order <= 512 or order % 2 != 0:
        lower = jnp.linalg.cholesky(matrix)
        identity = jnp.eye(order, dtype=matrix.dtype)
        return lax.linalg.triangular_solve(lower, identity, left_side=True, lower=True)
    half = order // 2
    upper_inv = inverse_factor(matrix[:half, :half])
    below = jnp.dot(matrix[half:, :half], upper_inv.T, precision=lax.Precision.HIGHEST)
    schur = matrix[half:, half:] - jnp.dot(below, below.T, precision=lax.Precision.HIGHEST)
    lower_inv = inverse_factor(schur)
    corner = -jnp.dot(
        lower_inv,
        jnp.dot(below, upper_inv, precision=lax.Precision.HIGHEST),
        precision=lax.Precision.HIGHEST,
    )
    top = jnp.concatenate([upper_inv, jnp.zeros((half, order - half), matrix.dtype)], axis=1)
    bottom = jnp.concatenate([corner, lower_inv], axis=1)
    return jnp.concatenate([top, bottom], axis=0)


def slab_atoms(owner_slab, slab):
    atoms = owner_slab.shape[0]
    keyed = jnp.where(owner_slab == slab, 0, 1) * atoms + jnp.arange(atoms, dtype=jnp.int32)
    return jnp.argsort(keyed, stable=True)[:A_SLAB]


def atom_terms(source, weights, starts, counts, coefs, valid):

    def take_rows(offset):
        return lax.dynamic_slice_in_dim(source, offset, SPH, 0)

    sphere_rows = jax.vmap(take_rows)(starts)
    correlations = jnp.einsum(
        "aij,ajn->ain", weights, sphere_rows, preferred_element_type=jnp.float32
    )
    active = (jnp.arange(NPMAX)[None, :] < counts[:, None]) & valid[:, None]
    correlations = jnp.where(active[:, :, None], correlations, jnp.zeros_like(correlations))
    weighted = jnp.einsum("aij,ajn->ain", coefs, correlations, precision=lax.Precision.HIGHEST)
    return (correlations, weighted)


def shards(orbitals, projectors, sphere_start, proj_count, owner_slab, correlation_coef):
    band_index = lax.axis_index("band")
    slab = lax.axis_index("grid")
    nbands = lax.axis_size("band")
    total_rows = orbitals.shape[0] * lax.axis_size("grid")
    chosen = slab_atoms(owner_slab, slab)
    weights = projectors[chosen]
    counts = proj_count[chosen]
    coefs = correlation_coef[chosen]
    gathered = lax.all_gather(orbitals, "band", axis=1, tiled=True)
    width = orbitals.shape[1]
    width_all = gathered.shape[1]
    gram_panel = jnp.dot(orbitals.T, gathered, preferred_element_type=jnp.float32) * (
        1.0 / total_rows
    )
    valid = jnp.ones((A_SLAB,), dtype=bool)
    correlations, weighted = atom_terms(
        gathered, weights, sphere_start[chosen], counts, coefs, valid
    )
    panel_weighted = lax.dynamic_slice_in_dim(weighted, band_index * width, width, 2)
    paw = jnp.dot(
        panel_weighted.reshape(-1, width).T,
        correlations.reshape(-1, width_all),
        precision=lax.Precision.HIGHEST,
    )
    panel_total = lax.psum(gram_panel + paw, "grid")
    metric = lax.all_gather(panel_total, "band", axis=0, tiled=True)
    height = orbitals.shape[0] // nbands
    mine = lax.dynamic_slice_in_dim(gathered, band_index * height, height, 0)
    inverse = inverse_factor(metric).astype(jnp.bfloat16)
    return jnp.dot(mine, inverse.T, preferred_element_type=jnp.float32).astype(jnp.bfloat16)


def solution(mesh):
    in_specs = (P("grid", "band"), P(), P(), P(), P(), P())
    out_specs = P(("grid", "band"), None)
    return jax.shard_map(shards, mesh=mesh, in_specs=in_specs, out_specs=out_specs, check_vma=False)
```

profile of v0, /device:TPU:1, one launch (start us, length us, event | category | flops | bytes accessed | tf_op | source)
XLA Modules:
  0.0 1023.9 jit_solution(12298596556159580187)
XLA Ops:
  15.4 50.7 %all-gather.3.cloned.1.call-done = bf16[2048,2048]{1,0:T(8,128)(2,1)} async-done(((bf16[2048,256]{1,0:T(8,128)(2,1)}), bf16[2048,2048]{1,0:T(8,128)(2,1)}) %all-gather.3.cloned.1.call-update) | async-done | bytes 8388624 | tf_op jit(solution)/shard_map/all_gather | solution.py:62
  66.1 25.7 %while.9 = (s32[]{:T(128)}, bf16[2048,2048]{1,0:T(8,128)(2,1)}, s32[8,2]{0,1:T(2,128)S(1)}, bf16[8,128,2048]{2,1,0:T(8,128)(2,1)}, s32[]{:T(128)}) while((s32[]{:T(128)}, bf16[2048,2048]{1,0:T(8,128)(2,1)}, s32[8,2]{0,1:T(2,128)S(1)}, bf16[8,128,2048]{2,1,0:T(8,128)(2,1)}, s32[]{:T(128)}) %tuple.104), condition=%wide.while_cond.1, body=%wide.while_body.1.sunk | while | flops 2 | bytes 1049189 | solution.py:41
  105.5 90.3 %all-reduce.7.cloned.1.call-done = f32[256,2048]{0,1:T(8,128)} async-done(((f32[256,2048]{0,1:T(8,128)}), f32[256,2048]{0,1:T(8,128)}) %all-reduce.7.cloned.1.call-update) | async-done | bytes 2097168 | tf_op jit(solution)/shard_map/psum | solution.py:78
  196.0 87.6 %all-gather.5.cloned.1.call-done = f32[2048,2048]{0,1:T(8,128)} async-done(((f32[256,2048]{0,1:T(8,128)}), f32[2048,2048]{0,1:T(8,128)}) %all-gather.5.cloned.1.call-update) | async-done | bytes 16777232 | tf_op jit(solution)/shard_map/all_gather | solution.py:79
  286.7 11.7 %cholesky.462 = f32[128,128]{1,0:T(8,128)S(1)} custom-call(f32[128,128]{1,0:T(8,128)S(1)} %cholesky.746), custom_call_target="Cholesky" | custom-call | tf_op jit(solution)/shard_map/jit(cholesky)/cholesky | solution.py:14
  309.1 11.7 %cholesky.481 = f32[128,128]{1,0:T(8,128)S(1)} custom-call(f32[128,128]{1,0:T(8,128)S(1)} %cholesky.750), custom_call_target="Cholesky" | custom-call | tf_op jit(solution)/shard_map/jit(cholesky)/cholesky | solution.py:14
  331.8 11.7 %cholesky.502 = f32[128,128]{1,0:T(8,128)S(1)} custom-call(f32[128,128]{1,0:T(8,128)S(1)} %cholesky.755), custom_call_target="Cholesky" | custom-call | tf_op jit(solution)/shard_map/jit(cholesky)/cholesky | solution.py:14
  353.9 11.7 %cholesky.519 = f32[128,128]{1,0:T(8,128)S(1)} custom-call(f32[128,128]{1,0:T(8,128)S(1)} %convolution_subtract_fusion.25), custom_call_target="Cholesky" | custom-call | tf_op jit(solution)/shard_map/jit(cholesky)/cholesky | solution.py:14
  378.1 39.3 %custom-call.38 = f32[4,128,128]{1,2,0:T(8,128)S(1)} custom-call(f32[4,128,128]{2,1,0:T(8,128)S(1)} %get-tuple-element.43), custom_call_target="InvertDiagBlocksLowerTriangular" | custom-call | tf_op jit(solution)/shard_map/triangular_solve/custom-call.3 | solution.py:16
  435.1 12.1 %cholesky.534 = f32[128,128]{1,0:T(8,128)S(1)} custom-call(f32[128,128]{1,0:T(8,128)S(1)} %cholesky.759), custom_call_target="Cholesky" | custom-call | tf_op jit(solution)/shard_map/jit(cholesky)/cholesky | solution.py:14
  459.7 11.7 %cholesky.553 = f32[128,128]{1,0:T(8,128)S(1)} custom-call(f32[128,128]{1,0:T(8,128)S(1)} %cholesky.763), custom_call_target="Cholesky" | custom-call | tf_op jit(solution)/shard_map/jit(cholesky)/cholesky | solution.py:14
  482.8 11.9 %cholesky.574 = f32[128,128]{1,0:T(8,128)S(1)} custom-call(f32[128,128]{1,0:T(8,128)S(1)} %cholesky.768), custom_call_target="Cholesky" | custom-call | tf_op jit(solution)/shard_map/jit(cholesky)/cholesky | solution.py:14
  506.0 11.7 %cholesky.591 = f32[128,128]{1,0:T(8,128)S(1)} custom-call(f32[128,128]{1,0:T(8,128)S(1)} %convolution_subtract_fusion.24), custom_call_target="Cholesky" | custom-call | tf_op jit(solution)/shard_map/jit(cholesky)/cholesky | solution.py:14
  535.1 39.5 %custom-call.42 = f32[4,128,128]{1,2,0:T(8,128)S(1)} custom-call(f32[4,128,128]{2,1,0:T(8,128)S(1)} %get-tuple-element.44), custom_call_target="InvertDiagBlocksLowerTriangular" | custom-call | tf_op jit(solution)/shard_map/triangular_solve/custom-call.3 | solution.py:16
  590.3 28.5 %fusion.9 = f32[1024,1024]{1,0:T(8,128)S(1)} fusion(f32[2048,2048]{0,1:T(8,128)} %all-gather.5.cloned.1.call-done, f32[512,512]{1,0:T(8,128)S(1)} %copy-done.5, f32[128,512]{1,0:T(8,128)S(1)} %fusion.125, f32[128,512]{1,0:T(8,128)S(1)} %fusion.126, f32[128,512]{1,0:T(8,128)S(1)} %fusion.128, f32[128,512]{1,0:T(8,128)S(1)} %fusion.81, ...), kind=kOutput, calls=%fused_computation.24 | convolution fusion | flops 12892241920 | bytes 11534336 | tf_op jit(solution)/shard_map/dot_general | solution.py:19
  618.8 18.2 %slice_subtract_fusion = f32[1024,1024]{0,1:T(8,128)} fusion(f32[2048,2048]{0,1:T(8,128)} %all-gather.5.cloned.1.call-done, f32[1024,1024]{1,0:T(8,128)S(1)} %fusion.9), kind=kOutput, calls=%fused_computation.26 | convolution fusion | flops 12885950464 | bytes 16777216 | tf_op jit(solution)/shard_map/dot_general | solution.py:20
  643.3 11.7 %cholesky.606 = f32[128,128]{1,0:T(8,128)S(1)} custom-call(f32[128,128]{1,0:T(8,128)S(1)} %cholesky.772), custom_call_target="Cholesky" | custom-call | tf_op jit(solution)/shard_map/jit(cholesky)/cholesky | solution.py:14
  667.5 11.7 %cholesky.625 = f32[128,128]{1,0:T(8,128)S(1)} custom-call(f32[128,128]{1,0:T(8,128)S(1)} %cholesky.776), custom_call_target="Cholesky" | custom-call | tf_op jit(solution)/shard_map/jit(cholesky)/cholesky | solution.py:14
  744.1 39.3 %custom-call.46 = f32[4,128,128]{1,2,0:T(8,128)S(1)} custom-call(f32[4,128,128]{2,1,0:T(8,128)S(1)} %get-tuple-element.45), custom_call_target="InvertDiagBlocksLowerTriangular" | custom-call | tf_op jit(solution)/shard_map/triangular_solve/custom-call.3 | solution.py:16
  801.2 17.2 %fusion.172 = f32[1024,1024]{1,0:T(8,128)} fusion(f32[1024,1024]{1,0:T(8,128)S(1)} %copy-done.17, f32[512,512]{1,0:T(8,128)S(1)} %copy-done.6, f32[128,512]{1,0:T(8,128)S(1)} %copy-done.12, f32[128,512]{1,0:T(8,128)S(1)} %fusion.126, f32[128,512]{1,0:T(8,128)S(1)} %fusion.128, f32[128,512]{1,0:T(8,128)S(1)} %fusion.81, f32[512,512]{1,0:T(8,128)S(1)} %copy-done.3), kind=kOutput, calls=%fused_computation.324 | convolution fusion | flops 12892241920 | bytes 11534336 | tf_op jit(solution)/shard_map/dot_general | solution.py:24
  911.2 12.0 %while.13 = (s32[]{:T(128)}, f32[512,512]{1,0:T(8,128)}, s32[4,2]{0,1:T(2,128)S(1)}, f32[4,128,128]{2,1,0:T(8,128)S(1)}, s32[]{:T(128)}) while((s32[]{:T(128)}, f32[512,512]{1,0:T(8,128)}, s32[4,2]{0,1:T(2,128)S(1)}, f32[4,128,128]{2,1,0:T(8,128)S(1)}, s32[]{:T(128)}) %tuple.127), condition=%wide.while_cond.clone.2, body=%wide.while_body.clone.2.sunk | while | flops 2 | bytes 131189 | solution.py:16
  923.2 39.3 %custom-call.50 = f32[4,128,128]{1,2,0:T(8,128)S(1)} custom-call(f32[4,128,128]{2,1,0:T(8,128)S(1)} %get-tuple-element.46), custom_call_target="InvertDiagBlocksLowerTriangular" | custom-call | tf_op jit(solution)/shard_map/triangular_solve/custom-call.3 | solution.py:16
  976.3 13.6 %negate_convert_fusion = bf16[1024,1024]{1,0:T(8,128)(2,1)S(1)} fusion(f32[1024,1024]{1,0:T(8,128)S(1)} %copy-done.18, f32[512,512]{1,0:T(8,128)S(1)} %copy-done.7, f32[128,512]{1,0:T(8,128)S(1)} %fusion.113, f32[128,512]{1,0:T(8,128)S(1)} %fusion.114, f32[128,512]{1,0:T(8,128)S(1)} %fusion.116, f32[128,512]{1,0:T(8,128)S(1)} %fusion.77, ...), kind=kOutput, calls=%fused_computation.30 | convolution fusion | flops 12894339072 | bytes 9437184 | tf_op jit(solution)/shard_map/dot_general | solution.py:22
  990.0 26.9 %fusion.13 = bf16[256,2048]{1,0:T(8,128)(2,1)} fusion(bf16[1024,1024]{1,0:T(8,128)(2,1)S(1)} %copy-done.13, bf16[1024,1024]{1,0:T(8,128)(2,1)S(1)} %fusion.16, bf16[1024,1024]{1,0:T(8,128)(2,1)S(1)} %negate_convert_fusion, bf16[2048,2048]{1,0:T(8,128)(2,1)} %get-tuple-element.377, s32[]{:T(128)S(6)} %select_n.31), kind=kOutput, calls=%fused_computation.34 | convolution fusion | flops 2181562368 | bytes 8388612 | tf_op jit(solution)/shard_map/dot_general | solution.py:83
  (287 shorter events, 420.8 us)
Async XLA Ops:
  6.5 4.0 copy-start
  6.5 59.5 %all-gather.3.cloned.1.call-start = ((), (), s32[]{:S(2)}) async-start(), calls=%async_computation | async-start | bytes 9437184 | tf_op jit(solution)/shard_map/all_gather | solution.py:62
  7.3 188.6 %all-reduce.7.cloned.1.call-start = ((), (), s32[]{:S(2)}) async-start(), calls=%async_computation.1 | async-start | bytes 4194304 | tf_op jit(solution)/shard_map/psum | solution.py:78
  91.7 3.5 copy-start.14
  105.3 178.4 %all-gather.5.cloned.1.call-start = ((), (), s32[]{:S(2)}) async-start(), calls=%async_computation.2 | async-start | bytes 18874368 | tf_op jit(solution)/shard_map/all_gather | solution.py:79
  434.1 1.0 copy-start.8
  574.7 3.5 copy-start.15
  575.1 8.2 copy-start.5
  581.4 8.8 copy-start.11
  583.3 35.5 %copy-start.2 = (f32[512,512]{1,0:T(8,128)}, f32[512,512]{1,0:T(8,128)S(1)}, u32[]{:S(2)}) copy-start(f32[512,512]{1,0:T(8,128)S(1)} %convolution_negate_fusion.1) | copy-start | bytes 3145732
  618.8 18.2 %copy-start.16 = (f32[1024,1024]{1,0:T(8,128)}, f32[1024,1024]{1,0:T(8,128)S(1)}, u32[]{:S(2)}) copy-start(f32[1024,1024]{1,0:T(8,128)S(1)} %fusion.9) | copy-start | bytes 12582916
  642.3 1.0 copy-start.10
  793.9 7.3 copy-start.3
  794.0 7.3 copy-start.6
  794.0 7.2 copy-start.12
  794.0 7.2 copy-start.17
  821.1 1.0 copy-start.9
  909.8 58.6 %copy-start.4 = (f32[512,512]{1,0:T(8,128)S(1)}, f32[512,512]{1,0:T(8,128)}, u32[]{:S(2)}) copy-start(f32[512,512]{1,0:T(8,128)} %fusion.170) | copy-start | bytes 3145732
  962.9 7.4 copy-start.7
  968.5 7.9 copy-start.18
  976.3 13.7 %copy-start.13 = (bf16[1024,1024]{1,0:T(8,128)(2,1)S(1)}, bf16[1024,1024]{1,0:T(8,128)(2,1)}, u32[]{:S(2)}) copy-start(bf16[1024,1024]{1,0:T(8,128)(2,1)} %fusion.173) | copy-start | bytes 6291460
  990.0 26.9 %copy-start.1 = (bf16[128,8,128]{2,1,0:T(8,128)(2,1)S(1)}, bf16[128,8,128]{2,1,0:T(8,128)(2,1)}, u32[]{:S(2)}) copy-start(bf16[128,8,128]{2,1,0:T(8,128)(2,1)} %param.10) | copy-start | bytes 786436
Sparse Core Ops, SparseCore 0:
  9.0 57.0 all-gather.2
  105.4 90.4 all-reduce.6
  197.6 86.0 all-gather.4
where the time goes:
time: 1030 us; the launch traced here: 1020 us
  other arithmetic  503 us (49%)
  waiting for transfers between devices  229 us (22%)
  matrix products  182 us (18%)
  local copies, waits for them, and re-layouts  84.3 us (8%)
  between operations  25.2 us (2%)
    another operation x59, other arithmetic, inverse_factor(): lower = jnp.linalg.cholesky(matrix)  317 us
    another operation x11, other arithmetic, inverse_factor(): lax.linalg.triangular_solve(lower, identity, left_side=True, lower=True)  163 us
    psum x1, waiting for transfers between devices, shards(): panel_total = lax.psum(gram_panel + paw, 'grid')  90.3 us
    all_gather x1, waiting for transfers between devices, shards(): metric = lax.all_gather(panel_total, 'band', axis=0, tiled=True)  87.6 us
    all_gather x1, waiting for transfers between devices, shards(): gathered = lax.all_gather(orbitals, 'band', axis=1, tiled=True)  50.7 us
    another operation x53, local copies, waits for them, and re-layouts, inverse_factor(): lax.linalg.triangular_solve(lower, identity, left_side=True, lower=True)  42.3 us
    dot_general x3, matrix products, inverse_factor(): jnp.dot(matrix[half:, :half], upper_inv.T, precision=lax.Precision.HIGHEST)  38 us
    dot_general x1, matrix products, shards(): jnp.dot(mine, inverse.T, preferred_element_type=jnp.float32)  26.9 us
  transfers between devices with their start and end apart: 3, of which 3 were waited for; matrix products, arithmetic and copies ran while one was open for 1% of the time, Pallas kernels for 0%

commit v1 on v0

--- a/solution.py
+++ b/solution.py
@@ -6,6 +6,12 @@
 SPH = 128
 NPMAX = 8
 A_SLAB = 8
+
+
+def add_all(x, axis):
+    parts = lax.all_gather(x, axis, axis=0, tiled=False)
+    total = parts.sum(axis=0)
+    return total
 
 
 def inverse_factor(matrix):
@@ -75,7 +81,7 @@
         correlations.reshape(-1, width_all),
         precision=lax.Precision.HIGHEST,
     )
-    panel_total = lax.psum(gram_panel + paw, "grid")
+    panel_total = add_all(gram_panel + paw, "grid")
     metric = lax.all_gather(panel_total, "band", axis=0, tiled=True)
     height = orbitals.shape[0] // nbands
     mine = lax.dynamic_slice_in_dim(gathered, band_index * height, height, 0)

time: 1030 us -> 1140 us (1.11)
  waiting for transfers between devices: 229 us -> 334 us
  other arithmetic: 503 us -> 515 us
    all_gather x0 -> x1, waiting for transfers between devices: none -> 198 us  [add_all(): parts = lax.all_gather(x, axis, axis=0, tiled=False)]
    psum x1 -> x0, waiting for transfers between devices: 90.3 us -> none  [shards(): panel_total = lax.psum(gram_panel + paw, 'grid')]
    reduce_sum x0 -> x1, other arithmetic: none -> 11.8 us  [add_all(): total = parts.sum(axis=0)]
where the time goes in v1:
time: 1140 us; the launch traced here: 1130 us
  other arithmetic  515 us (45%)
  waiting for transfers between devices  334 us (29%)
  matrix products  173 us (15%)
  local copies, waits for them, and re-layouts  87.8 us (8%)
  between operations  25.2 us (2%)
    another operation x59, other arithmetic, inverse_factor(): lower = jnp.linalg.cholesky(matrix)  317 us
    all_gather x1, waiting for transfers between devices, add_all(): parts = lax.all_gather(x, axis, axis=0, tiled=False)  198 us
    another operation x11, other arithmetic, inverse_factor(): lax.linalg.triangular_solve(lower, identity, left_side=True, lower=True)  163 us
    all_gather x1, waiting for transfers between devices, shards(): metric = lax.all_gather(panel_total, 'band', axis=0, tiled=True)  85 us
    all_gather x1, waiting for transfers between devices, shards(): gathered = lax.all_gather(orbitals, 'band', axis=1, tiled=True)  50.7 us
    another operation x53, local copies, waits for them, and re-layouts, inverse_factor(): lax.linalg.triangular_solve(lower, identity, left_side=True, lower=True)  42.9 us
    dot_general x3, matrix products, inverse_factor(): jnp.dot(matrix[half:, :half], upper_inv.T, precision=lax.Precision.HIGHEST)  36.9 us
    dot_general x1, matrix products, shards(): jnp.dot(mine, inverse.T, preferred_element_type=jnp.float32)  26.8 us
  transfers between devices with their start and end apart: 3, of which 3 were waited for; matrix products, arithmetic and copies ran while one was open for 1% of the time, Pallas kernels for 0%

profile of v1, /device:TPU:1, one launch (start us, length us, event | category | flops | bytes accessed | tf_op | source)
XLA Modules:
  0.0 1134.8 jit_solution(5611784396676347777)
XLA Ops:
  15.4 50.7 %all-gather.5.cloned.1.call-done = bf16[2048,2048]{1,0:T(8,128)(2,1)} async-done(((bf16[2048,256]{1,0:T(8,128)(2,1)}), bf16[2048,2048]{1,0:T(8,128)(2,1)}) %all-gather.5.cloned.1.call-update) | async-done | bytes 8388624 | tf_op jit(solution)/shard_map/all_gather | solution.py:68
  66.1 25.9 %while.9 = (s32[]{:T(128)}, bf16[2048,2048]{1,0:T(8,128)(2,1)}, s32[8,2]{0,1:T(2,128)S(1)}, bf16[8,128,2048]{2,1,0:T(8,128)(2,1)}, s32[]{:T(128)}) while((s32[]{:T(128)}, bf16[2048,2048]{1,0:T(8,128)(2,1)}, s32[8,2]{0,1:T(2,128)S(1)}, bf16[8,128,2048]{2,1,0:T(8,128)(2,1)}, s32[]{:T(128)}) %tuple.104), condition=%wide.while_cond.1, body=%wide.while_body.1.sunk | while | flops 2 | bytes 1049689 | solution.py:47
  101.1 197.6 %all-gather.9.cloned.1.call-done = f32[4096,2048]{1,0:T(8,128)} async-done(((f32[256,2048]{1,0:T(8,128)}), f32[4096,2048]{1,0:T(8,128)}) %all-gather.9.cloned.1.call-update) | async-done | bytes 33554448 | tf_op jit(solution)/shard_map/all_gather | solution.py:12
  298.8 11.8 %reduce_sum.9 = f32[256,2048]{1,0:T(8,128)S(1)} reduce(f32[16,256,2048]{2,1,0:T(8,128)} %bitcast.223, f32[]{:T(128)} %constant.131.clone.1), dimensions={0}, to_apply=%region_1.2 | reduce | flops 7864320 | bytes 35651588 | tf_op jit(solution)/shard_map/reduce_sum | solution.py:13
  312.8 85.0 %all-gather.7.cloned.1.call-done = f32[2048,2048]{0,1:T(8,128)} async-done(((f32[256,2048]{0,1:T(8,128)}), f32[2048,2048]{0,1:T(8,128)}) %all-gather.7.cloned.1.call-update) | async-done | bytes 16777232 | tf_op jit(solution)/shard_map/all_gather | solution.py:85
  400.9 11.7 %cholesky.462 = f32[128,128]{1,0:T(8,128)S(1)} custom-call(f32[128,128]{1,0:T(8,128)S(1)} %cholesky.746), custom_call_target="Cholesky" | custom-call | tf_op jit(solution)/shard_map/jit(cholesky)/cholesky | solution.py:20
  423.3 11.7 %cholesky.481 = f32[128,128]{1,0:T(8,128)S(1)} custom-call(f32[128,128]{1,0:T(8,128)S(1)} %cholesky.750), custom_call_target="Cholesky" | custom-call | tf_op jit(solution)/shard_map/jit(cholesky)/cholesky | solution.py:20
  445.9 11.7 %cholesky.502 = f32[128,128]{1,0:T(8,128)S(1)} custom-call(f32[128,128]{1,0:T(8,128)S(1)} %cholesky.755), custom_call_target="Cholesky" | custom-call | tf_op jit(solution)/shard_map/jit(cholesky)/cholesky | solution.py:20
  468.7 11.7 %cholesky.519 = f32[128,128]{1,0:T(8,128)S(1)} custom-call(f32[128,128]{1,0:T(8,128)S(1)} %convolution_subtract_fusion.25), custom_call_target="Cholesky" | custom-call | tf_op jit(solution)/shard_map/jit(cholesky)/cholesky | solution.py:20
  492.8 39.3 %custom-call.38 = f32[4,128,128]{1,2,0:T(8,128)S(1)} custom-call(f32[4,128,128]{2,1,0:T(8,128)S(1)} %get-tuple-element.43), custom_call_target="InvertDiagBlocksLowerTriangular" | custom-call | tf_op jit(solution)/shard_map/triangular_solve/custom-call.3 | solution.py:22
  549.8 12.1 %cholesky.534 = f32[128,128]{1,0:T(8,128)S(1)} custom-call(f32[128,128]{1,0:T(8,128)S(1)} %cholesky.759), custom_call_target="Cholesky" | custom-call | tf_op jit(solution)/shard_map/jit(cholesky)/cholesky | solution.py:20
  574.4 11.7 %cholesky.553 = f32[128,128]{1,0:T(8,128)S(1)} custom-call(f32[128,128]{1,0:T(8,128)S(1)} %cholesky.763), custom_call_target="Cholesky" | custom-call | tf_op jit(solution)/shard_map/jit(cholesky)/cholesky | solution.py:20
  598.9 11.9 %cholesky.574 = f32[128,128]{1,0:T(8,128)S(1)} custom-call(f32[128,128]{1,0:T(8,128)S(1)} %cholesky.768), custom_call_target="Cholesky" | custom-call | tf_op jit(solution)/shard_map/jit(cholesky)/cholesky | solution.py:20
  622.8 11.7 %cholesky.591 = f32[128,128]{1,0:T(8,128)S(1)} custom-call(f32[128,128]{1,0:T(8,128)S(1)} %convolution_subtract_fusion.24), custom_call_target="Cholesky" | custom-call | tf_op jit(solution)/shard_map/jit(cholesky)/cholesky | solution.py:20
  650.4 39.3 %custom-call.42 = f32[4,128,128]{1,2,0:T(8,128)S(1)} custom-call(f32[4,128,128]{2,1,0:T(8,128)S(1)} %get-tuple-element.44), custom_call_target="InvertDiagBlocksLowerTriangular" | custom-call | tf_op jit(solution)/shard_map/triangular_solve/custom-call.3 | solution.py:22
  698.4 28.6 %fusion.9 = f32[1024,1024]{1,0:T(8,128)S(1)} fusion(f32[2048,2048]{0,1:T(8,128)} %all-gather.7.cloned.1.call-done, f32[512,512]{1,0:T(8,128)S(1)} %copy-done.7, f32[128,512]{1,0:T(8,128)S(1)} %fusion.125, f32[128,512]{1,0:T(8,128)S(1)} %fusion.126, f32[128,512]{1,0:T(8,128)S(1)} %fusion.128, f32[128,512]{1,0:T(8,128)S(1)} %fusion.81, ...), kind=kOutput, calls=%fused_computation.24 | convolution fusion | flops 12892241920 | bytes 11534336 | tf_op jit(solution)/shard_map/dot_general | solution.py:25
  727.0 16.8 %fusion.172 = f32[1024,1024]{1,0:T(8,128)} fusion(f32[1024,1024]{1,0:T(8,128)S(1)} %fusion.9, f32[512,512]{1,0:T(8,128)S(1)} %copy-done.7, f32[128,512]{1,0:T(8,128)S(1)} %fusion.125, f32[128,512]{1,0:T(8,128)S(1)} %fusion.126, f32[128,512]{1,0:T(8,128)S(1)} %fusion.128, f32[128,512]{1,0:T(8,128)S(1)} %fusion.81, f32[512,512]{1,0:T(8,128)S(1)} %convolution_negate_fusion.1), kind=kOutput, calls=%fused_computation.324 | convolution fusion | flops 12892241920 | bytes 11534336 | tf_op jit(solution)/shard_map/dot_general | solution.py:30
  743.8 16.0 %slice_subtract_fusion = f32[1024,1024]{0,1:T(8,128)S(1)} fusion(f32[2048,2048]{0,1:T(8,128)} %all-gather.7.cloned.1.call-done, f32[1024,1024]{1,0:T(8,128)S(1)} %fusion.9), kind=kOutput, calls=%fused_computation.26 | convolution fusion | flops 12885950464 | bytes 16777216 | tf_op jit(solution)/shard_map/dot_general | solution.py:26
  856.0 11.8 %while.12 = (s32[]{:T(128)}, f32[512,512]{1,0:T(8,128)}, s32[4,2]{0,1:T(2,128)S(1)}, f32[4,128,128]{2,1,0:T(8,128)S(1)}, s32[]{:T(128)}) while((s32[]{:T(128)}, f32[512,512]{1,0:T(8,128)}, s32[4,2]{0,1:T(2,128)S(1)}, f32[4,128,128]{2,1,0:T(8,128)S(1)}, s32[]{:T(128)}) %tuple.126), condition=%wide.while_cond.clone.1, body=%wide.while_body.clone.1.sunk | while | flops 2 | bytes 131181 | solution.py:22
  867.9 39.3 %custom-call.46 = f32[4,128,128]{1,2,0:T(8,128)S(1)} custom-call(f32[4,128,128]{2,1,0:T(8,128)S(1)} %get-tuple-element.45), custom_call_target="InvertDiagBlocksLowerTriangular" | custom-call | tf_op jit(solution)/shard_map/triangular_solve/custom-call.3 | solution.py:22
  1022.6 11.8 %while.13 = (s32[]{:T(128)}, f32[512,512]{1,0:T(8,128)}, s32[4,2]{0,1:T(2,128)S(1)}, f32[4,128,128]{2,1,0:T(8,128)S(1)}, s32[]{:T(128)}) while((s32[]{:T(128)}, f32[512,512]{1,0:T(8,128)}, s32[4,2]{0,1:T(2,128)S(1)}, f32[4,128,128]{2,1,0:T(8,128)S(1)}, s32[]{:T(128)}) %tuple.127), condition=%wide.while_cond.clone.2, body=%wide.while_body.clone.2.sunk | while | flops 2 | bytes 131181 | solution.py:22
  1034.4 39.3 %custom-call.50 = f32[4,128,128]{1,2,0:T(8,128)S(1)} custom-call(f32[4,128,128]{2,1,0:T(8,128)S(1)} %get-tuple-element.46), custom_call_target="InvertDiagBlocksLowerTriangular" | custom-call | tf_op jit(solution)/shard_map/triangular_solve/custom-call.3 | solution.py:22
  1087.5 13.6 %negate_convert_fusion = bf16[1024,1024]{1,0:T(8,128)(2,1)S(1)} fusion(f32[1024,1024]{1,0:T(8,128)S(1)} %copy-done.19, f32[512,512]{1,0:T(8,128)S(1)} %copy-done.9, f32[128,512]{1,0:T(8,128)S(1)} %fusion.113, f32[128,512]{1,0:T(8,128)S(1)} %fusion.114, f32[128,512]{1,0:T(8,128)S(1)} %fusion.116, f32[128,512]{1,0:T(8,128)S(1)} %fusion.77, ...), kind=kOutput, calls=%fused_computation.30 | convolution fusion | flops 12894339072 | bytes 9437184 | tf_op jit(solution)/shard_map/dot_general | solution.py:28
  1101.1 26.8 %fusion.13 = bf16[256,2048]{1,0:T(8,128)(2,1)} fusion(bf16[1024,1024]{1,0:T(8,128)(2,1)S(1)} %copy-done.17, bf16[1024,1024]{1,0:T(8,128)(2,1)S(1)} %fusion.16, bf16[1024,1024]{1,0:T(8,128)(2,1)S(1)} %negate_convert_fusion, bf16[2048,2048]{1,0:T(8,128)(2,1)} %get-tuple-element.366, s32[]{:T(128)S(6)} %select_n.31), kind=kOutput, calls=%fused_computation.34 | convolution fusion | flops 2181562368 | bytes 8388612 | tf_op jit(solution)/shard_map/dot_general | solution.py:89
  (291 shorter events, 430.3 us)
Async XLA Ops:
  6.5 5.3 copy-start
  6.5 59.5 %all-gather.5.cloned.1.call-start = ((), (), s32[]{:S(2)}) async-start(), calls=%async_computation | async-start | bytes 9437184 | tf_op jit(solution)/shard_map/all_gather | solution.py:68
  7.3 291.5 %all-gather.9.cloned.1.call-start = ((), (), s32[]{:S(2)}) async-start(), calls=%async_computation.2 | async-start | bytes 35651584 | tf_op jit(solution)/shard_map/all_gather | solution.py:12
  91.9 5.4 copy-start.2
  94.9 2.4 copy-start.3
  101.1 296.7 %all-gather.7.cloned.1.call-start = ((), (), s32[]{:S(2)}) async-start(), calls=%async_computation.1 | async-start | bytes 18874368 | tf_op jit(solution)/shard_map/all_gather | solution.py:85
  548.9 1.0 copy-start.12
  689.7 3.5 copy-start.18
  690.2 8.2 copy-start.7
  696.5 30.5 %copy-start.15 = (f32[128,512]{1,0:T(8,128)}, f32[128,512]{1,0:T(8,128)S(1)}, u32[]{:S(2)}) copy-start(f32[128,512]{1,0:T(8,128)S(1)} %fusion.125) | copy-start | bytes 786436
  698.4 28.7 %copy-start.4 = (f32[512,512]{1,0:T(8,128)}, f32[512,512]{1,0:T(8,128)S(1)}, u32[]{:S(2)}) copy-start(f32[512,512]{1,0:T(8,128)S(1)} %convolution_negate_fusion.1) | copy-start | bytes 3145732
  759.9 2.0 copy-start.10
  765.9 1.0 copy-start.14
  907.2 7.1 copy-start.11
  917.8 4.8 copy-start.5
  917.9 4.8 copy-start.8
  917.9 4.8 copy-start.16
  932.6 1.0 copy-start.13
  1021.3 58.3 %copy-start.6 = (f32[512,512]{1,0:T(8,128)S(1)}, f32[512,512]{1,0:T(8,128)}, u32[]{:S(2)}) copy-start(f32[512,512]{1,0:T(8,128)} %fusion.170) | copy-start | bytes 3145732
  1074.1 7.4 copy-start.9
  1079.7 7.9 copy-start.19
  1087.5 13.6 %copy-start.17 = (bf16[1024,1024]{1,0:T(8,128)(2,1)S(1)}, bf16[1024,1024]{1,0:T(8,128)(2,1)}, u32[]{:S(2)}) copy-start(bf16[1024,1024]{1,0:T(8,128)(2,1)} %fusion.173) | copy-start | bytes 6291460
  1101.1 26.8 %copy-start.1 = (bf16[128,8,128]{2,1,0:T(8,128)(2,1)S(1)}, bf16[128,8,128]{2,1,0:T(8,128)(2,1)}, u32[]{:S(2)}) copy-start(bf16[128,8,128]{2,1,0:T(8,128)(2,1)} %param.10) | copy-start | bytes 786436
Sparse Core Ops, SparseCore 0:
  9.0 57.0 all-gather.4
  101.2 197.4 all-gather.8
  312.8 84.9 all-gather.6
